TPU v7x, 8 devices: a whole 2x2x1 slice. The times are simulated.
8 devices in a mesh: col: 2 (over z, y), row: 4 (over x, core).
Axes of the slice: x: 2, y: 2, z: 1, core: 2. Of those that a mesh axis runs over, the one named last changes fastest.
Arguments:
- img_emb: bfloat16 [8192, 512], P(('row', 'col'))
- txt_emb: bfloat16 [8192, 512], P(('row', 'col'))
- log_scale: float32 [], replicated
Outputs:
- output 1: float32 [], replicated
- output 2: bfloat16 [8192, 512], P(('row', 'col'))
- output 3: bfloat16 [8192, 512], P(('row', 'col'))
- output 4: float32 [], replicated
All inputs are finite; a program needn't handle non-finite values.
Results may differ from a plain program's by a relative error of at most 0.001.
Values are sent between devices in bfloat16 or wider.
A program may use at most 1 GiB of HBM per device.

v0:
```python
import functools
import math

import jax
import jax.numpy as jnp
from jax import lax
from jax.experimental import pallas as pl
from jax.experimental.pallas import tpu as pltpu
from jax.sharding import PartitionSpec as P

MESH = pl.DeviceIdType.MESH
VMEM_LIMIT = 247 * 256 * 1024
F32 = jnp.float32
BF16 = jnp.bfloat16
ROWS = 1024
DIM = 512
CHUNK = 256
STEPS = ROWS // CHUNK
SIZES = (2, 1, 2, 2, 2, 2, 2, 2, 1)
TXT_START = (0, 8, 2, 4, 6, 9, 11, 13, 15)
BULK = len(SIZES)
PIECE = 128
GATHER = (2, 2, 2, 1, 1)
G_START = tuple(sum(GATHER[:k]) for k in range(len(GATHER)))
G_STEPS = len(GATHER)
IMGS = 2 * ROWS
TXTS = 4 * ROWS
X_BASE = 2 * ROWS
LOG2E = math.log2(math.e)


def kernel(inv_count, scale_ref, img_hbm, txt_hbm, loss_ref, dimg_ref, dtxt_ref, dscale_ref,
           img, txt, far, txt_t, img_p, new_txt, new_img, exps, row_e, row_m, col_e, col_m, row_send, row_recv, col_send, col_recv, col_b, row_l, all_a, all_b, new_a, new_b, txt_b,
           scal, scal_y, load_sem, gy_send, gy_recv, gx_send, gx_recv, gp_sem, gf_send, gf_recv, row_sem, col_ssem, col_rsem,
           bx_send, bx_recv, by_send, by_recv, fx_send, fx_recv, fy_send, fy_recv, pn_send, pn_recv,
           a_ssem, a_rsem, b_sem, sc_ssem, sc_rsem):
    row = lax.axis_index("row")
    col = lax.axis_index("col")
    core = lax.rem(row, 2)
    partner = row + 1 - 2 * core
    across = lax.rem(row + 2, 4)
    diagonal = across + 1 - 2 * core
    peers = (partner, across, diagonal)
    other_col = 1 - col

    def to_y(src, dst, ssem, rsem):
        return pltpu.make_async_remote_copy(src, dst, ssem, rsem, device_id={"row": row, "col": other_col}, device_id_type=MESH)

    def to_row(src, dst, ssem, rsem, peer):
        return pltpu.make_async_remote_copy(src, dst, ssem, rsem, device_id={"row": peer, "col": col}, device_id_type=MESH)

    txt_pieces = txt.at[0].reshape(ROWS // PIECE, PIECE, DIM)
    loads = []
    for k in range(G_STEPS):
        part = pl.ds(G_START[k] * PIECE, GATHER[k] * PIECE)
        loads.append((pltpu.make_async_copy(txt_hbm.at[part], txt.at[0, part], load_sem.at[k]),
                      pltpu.make_async_copy(img_hbm.at[part], img.at[part], load_sem.at[G_STEPS + k])))
        for copy in loads[k]:
            copy.start()

    barrier = pltpu.get_barrier_semaphore()
    for peer in peers:
        pl.semaphore_signal(barrier, inc=1, device_id={"row": peer, "col": col}, device_id_type=MESH)
    pl.semaphore_signal(barrier, inc=1, device_id={"row": row, "col": other_col}, device_id_type=MESH)

    pl.semaphore_wait(barrier, 4)

    gather_y, gather_x, relay = [], [], []
    for k in range(G_STEPS):
        pieces = pl.ds(G_START[k], GATHER[k])
        part = pl.ds(G_START[k] * PIECE, GATHER[k] * PIECE)
        gather_x.append(to_row(txt_pieces.at[pieces], far.at[pieces, 0], gx_send.at[k], gx_recv.at[k], across))
        gather_y.append(to_y(img.at[part], img.at[pl.ds(ROWS + G_START[k] * PIECE, GATHER[k] * PIECE)], gy_send.at[k], gy_recv.at[k]))
        relay.append(to_row(far.at[pieces, 0], far.at[pieces, 1], gf_send.at[k], gf_recv.at[k], partner))
        loads[k][0].wait()
        gather_x[k].start()
        loads[k][1].wait()
        gather_y[k].start()
    gather_p = to_row(txt.at[0], txt.at[1], gp_sem.at[0], gp_sem.at[1], partner)
    gather_p.start()
    gather_i = to_row(img.at[pl.ds(0, ROWS)], img_p.at[pl.ds(0, ROWS)], gp_sem.at[2], gp_sem.at[3], partner)
    gather_i.start()
    relay_n = []
    for k in range(G_STEPS):
        part = pl.ds(ROWS + G_START[k] * PIECE, GATHER[k] * PIECE)
        relay_n.append(to_row(img.at[part], img_p.at[part], pn_send.at[k], pn_recv.at[k], partner))

    img_pieces = img.reshape(IMGS // PIECE, PIECE, DIM)
    new_img_pieces = new_img.reshape(TXTS // PIECE, PIECE, DIM)
    new_txt_pieces = new_txt.reshape(TXTS // PIECE, PIECE, DIM)

    def bulk_span(k):
        start = sum(SIZES[:k])
        return start, 2 * start, SIZES[k]

    bulk_x, bulk_y = [], []
    for k in range(BULK):
        src, dst, size = bulk_span(k)
        land = pl.ds(dst, size)
        bulk_x.append(to_row(img_pieces.at[pl.ds(src, size)], new_img_pieces.at[land], bx_send.at[k], bx_recv.at[k], across))
        half = ROWS // PIECE
        src = TXT_START[k]
        source = txt_pieces.at[pl.ds(src, size)] if src < half else far.at[pl.ds(src - half, size), 0]
        bulk_y.append(to_y(source, new_txt_pieces.at[land], by_send.at[k], by_recv.at[k]))
    bulk_x[0].start()
    bulk_y[0].start()
    bulk_x[1].start()

    scale = jnp.max(jnp.exp(jnp.full((8, 128), scale_ref[0, 0], F32)))
    scale2 = scale * LOG2E
    row_e[...] = jnp.zeros_like(row_e)
    row_m[...] = jnp.zeros_like(row_m)
    col_e[...] = jnp.zeros_like(col_e)
    col_m[...] = jnp.zeros_like(col_m)

    def logit_block(r0, nr, c0, nc, texts, on_rows, kept):
        rows = pl.ds(r0, nr)
        cols = pl.ds(c0, nc)
        dots = lax.dot_general(img[rows, :], texts, (((1,), (1 if on_rows else 0,)), ((), ())), preferred_element_type=F32)
        e = jnp.exp2(dots * scale2)
        if kept:
            exps[pl.ds(r0, kept), cols] = e[:kept]
        m = e * dots
        for values, row_sum, col_sum in ((e, row_e, col_e), (m, row_m, col_m)):
            acc = values[:, 0:128]
            for q in range(1, nc // 128):
                acc = acc + values[:, q * 128:(q + 1) * 128]
            row_sum[rows, :] += acc
            col_sum[:, cols] += jnp.sum(values.reshape(nr // 8, 8, nc), axis=0)

    def own_by_held(slot):
        def body(i, carry):
            part = pl.ds(pl.multiple_of(i * 512, 512), 512)
            logit_block(0, ROWS, pl.multiple_of(slot * ROWS + i * 512, 512), 512, txt[slot, part, :], True, ROWS)
            return carry
        lax.fori_loop(0, 2, body, 0)

    def turn_held(slot):
        def body(i, carry):
            part = pl.ds(pl.multiple_of(i * CHUNK, CHUNK), CHUNK)
            txt_t[:, pl.ds(pl.multiple_of(slot * ROWS + i * CHUNK, CHUNK), CHUNK)] = txt[slot, part, :].T
            return carry
        lax.fori_loop(0, STEPS, body, 0)

    def partner_exps(c0, n):
        dots = lax.dot_general(txt[0], img_p[pl.ds(c0, n), :], (((1,), (1,)), ((), ())), preferred_element_type=F32)
        exps[ROWS:, pl.ds(ROWS + c0, n)] = jnp.exp2(dots * scale2)

    own_by_held(0)
    turn_held(0)

    def diag_body(i, acc):
        part = pl.ds(pl.multiple_of(i * 128, 128), 128)
        prod = img[part, :].astype(F32) * txt[0, part, :].astype(F32)
        return acc + jnp.sum(prod.reshape(16, 8, DIM), axis=0)
    diag_sum = jnp.sum(lax.fori_loop(0, 8, diag_body, jnp.zeros((8, DIM), F32)))

    gather_p.wait_recv()
    own_by_held(1)
    turn_held(1)
    gather_i.wait_recv()
    def partner_own(i, carry):
        partner_exps(pl.multiple_of(i * 512, 512), 512)
        return carry
    lax.fori_loop(0, 2, partner_own, 0)
    for k in range(G_STEPS):
        n_rows = GATHER[k] * PIECE
        done = G_START[k] * PIECE
        new_row = ROWS + done
        gather_x[k].wait_recv()
        relay[k].start()
        if k == 0:
            bulk_y[1].start()
        gather_y[k].wait_recv()
        relay_n[k].start()
        def new_by_held(i, carry, new_row=new_row, n_rows=n_rows):
            c0 = pl.multiple_of(i * 1024, 1024)
            logit_block(new_row, n_rows, c0, 1024, txt_t[:, pl.ds(c0, 1024)], False, 0)
            return carry
        n_held = X_BASE + 2 * done
        logit_block(new_row, n_rows, 0, ROWS, txt_t[:, :ROWS], False, n_rows)
        lax.fori_loop(1, n_held // 1024, new_by_held, 0)
        if n_held % 1024:
            c0 = n_held // 1024 * 1024
            logit_block(new_row, n_rows, c0, n_held - c0, txt_t[:, c0:n_held], False, 0)
        relay[k].wait_recv()
        new_cols = 2 * n_rows
        logit_block(0, new_row + n_rows, n_held, new_cols, far[G_START[k]:G_START[k] + GATHER[k]].reshape(new_cols, DIM), True, ROWS)
        if k + 1 < G_STEPS:
            for p in range(G_START[k], G_START[k] + GATHER[k]):
                c0 = X_BASE + 2 * p * PIECE
                txt_t[:, c0:c0 + 2 * PIECE] = far[p].reshape(2 * PIECE, DIM).T
        if k < 3:
            relay_n[k].wait_recv()
            partner_exps(ROWS + k * CHUNK, CHUNK)

    row_send[...] = jnp.sum(row_e[...].T, axis=0, keepdims=True)
    col_send[...] = jnp.sum(col_e[...], axis=0, keepdims=True)
    swap_row = to_y(row_send, row_recv, row_sem.at[0], row_sem.at[1])
    swap_row.start()
    swap_col = []
    for t, peer in enumerate(peers):
        swap_col.append(to_row(col_send, col_recv.at[t], col_ssem.at[t], col_rsem.at[t], peer))
        swap_col[t].start()
    bulk_x[2].start()
    bulk_y[2].start()
    relay_n[3].wait_recv()
    relay_n[4].wait_recv()
    partner_exps(ROWS + 3 * CHUNK, CHUNK)
    swap_row.wait_recv()
    row_tot = row_send[...] + jnp.concatenate([row_recv[:, ROWS:], row_recv[:, :ROWS]], axis=1)
    row_a = row_e
    row_l[...] = inv_count / row_tot
    swap_a = []
    for t, peer in enumerate(peers):
        swap_a.append(to_row(row_l, all_a.at[t], a_ssem.at[t], a_rsem.at[t], peer))
        swap_a[t].start()
    row_a[...] = jnp.broadcast_to(row_l[...], (128, IMGS)).T
    for t in range(3):
        swap_col[t].wait_recv()
    def slot(ref, s):
        if s < 2:
            return ref[:, s * ROWS:(s + 1) * ROWS]
        starts = [X_BASE + (2 * p + s - 2) * PIECE for p in range(ROWS // PIECE)]
        return jnp.concatenate([ref[:, c:c + PIECE] for c in starts], axis=1)
    for s in range(4):
        tot = (slot(col_send, s) + slot(col_recv.at[0], s ^ 1)) + (slot(col_recv.at[1], s ^ 2) + slot(col_recv.at[2], s ^ 3))
        inverse = inv_count / tot
        if s < 2:
            col_b[:, s * ROWS:(s + 1) * ROWS] = inverse
        else:
            for p in range(ROWS // PIECE):
                start = X_BASE + (2 * p + s - 2) * PIECE
                col_b[:, start:start + PIECE] = inverse[:, p * PIECE:(p + 1) * PIECE]

    def d_img_chunk(r0):
        rows = pl.ds(r0, CHUNK)
        total = None
        for j in range(TXTS // 512):
            g = [exps[rows, c:c + 128] * (row_a[rows, :] + col_b[:, c:c + 128]) for c in range(j * 512, (j + 1) * 512, 128)]
            g = jnp.concatenate([v.astype(BF16) for v in g], axis=1)
            texts = txt[j // 2, j % 2 * 512:(j % 2 + 1) * 512, :] if j < 4 else far[2 * j - 8:2 * j - 6].reshape(512, DIM)
            part = jnp.dot(g, texts, preferred_element_type=F32)
            total = part if total is None else total + part
        return total

    def d_txt_chunk(starts):
        total = None
        for i in range(IMGS // 512):
            rows = slice(i * 512, (i + 1) * 512)
            g = []
            for start in starts:
                cols = pl.ds(start, PIECE)
                g.append((exps[rows, cols] * (row_a[rows, :] + col_b[:, cols])).astype(BF16))
            g = jnp.concatenate(g, axis=1)
            part = lax.dot_general(g, img[rows, :], (((0,), (0,)), ((), ())), preferred_element_type=F32)
            total = part if total is None else total + part
        return total

    swap_b = to_y(col_b, all_b, b_sem.at[0], b_sem.at[1])
    swap_b.start()
    own_r = row_send[:, :ROWS] + row_recv[:, ROWS:]
    loss_part = jnp.sum(jnp.log(own_r) - jnp.log(col_b[:, :ROWS] / inv_count)) - 2.0 * scale * diag_sum
    dscale_part = scale * (jnp.sum(row_a[...] * row_m[...]) + jnp.sum(jnp.sum(col_m[...], axis=0, keepdims=True) * col_b[...])
                           - 2.0 * inv_count * diag_sum)
    lane = lax.broadcasted_iota(jnp.int32, (8, 128), 1)
    scal[0] = jnp.where(lane == 0, loss_part * inv_count, dscale_part)
    send_s = [to_row(scal.at[0], scal.at[t + 1], sc_ssem.at[t], sc_rsem.at[t], peer) for t, peer in enumerate(peers)]
    for t in range(3):
        send_s[t].start()
    for k in range(3, BULK):
        bulk_x[k].start()
        bulk_y[k].start()

    corner = IMGS + ROWS
    d_img_acc = exps.at[pl.ds(ROWS, ROWS), pl.ds(corner, DIM)]
    d_txt_acc = exps.at[pl.ds(ROWS, ROWS), pl.ds(corner + DIM, DIM)]

    def fix_body(i, carry):
        part = pl.ds(pl.multiple_of(i * 128, 128), 128)
        on_diag = lax.broadcasted_iota(jnp.int32, (128, 128), 0) == lax.broadcasted_iota(jnp.int32, (128, 128), 1)
        term = (2.0 * inv_count) / (row_a[part, :] + col_b[:, part])
        exps[part, part] = exps[part, part] - jnp.where(on_diag, term, 0.0)
        return carry
    lax.fori_loop(0, ROWS // 128, fix_body, 0)
    txt_b[...] = jnp.broadcast_to(col_b[:, :ROWS], (128, ROWS)).T

    def tile_body(k, carry):
        first = pl.multiple_of(k * CHUNK, CHUNK)
        part = pl.ds(first, CHUNK)
        d_img_acc[part, :] = d_img_chunk(first)
        d_txt_acc[part, :] = d_txt_chunk((first, first + PIECE))
        return carry
    lax.fori_loop(0, STEPS, tile_body, 0)

    for t in range(3):
        swap_a[t].wait_recv()
        send_s[t].wait_recv()
    swap_b.wait_recv()
    direct_b = jnp.concatenate([slot(all_b, 0), slot(all_b, 2)], axis=1)
    relayed_b = jnp.concatenate([slot(all_b, 1), slot(all_b, 3)], axis=1)
    for k in range(BULK):
        src_a, dst, size = (PIECE * v for v in bulk_span(k))
        src_b = PIECE * TXT_START[k]
        for to, direct, relayed, src in ((new_a, all_a[1], all_a[2], src_a), (new_b, direct_b, relayed_b, src_b)):
            to[:, dst:dst + size] = direct[:, src:src + size]
            to[:, dst + size:dst + 2 * size] = relayed[:, src:src + size]
    scal_y[0] = (scal[0] + scal[1]) + (scal[2] + scal[3])
    swap_s = to_y(scal_y.at[0], scal_y.at[1], sc_ssem.at[3], sc_rsem.at[3])
    swap_s.start()

    def partner_body(k, carry):
        first = pl.multiple_of(k * CHUNK, CHUNK)
        part = pl.ds(first, CHUNK)
        low = pl.ds(ROWS + first, CHUNK)
        total = None
        for j in range(IMGS // 512):
            g = [exps[low, ROWS + c:ROWS + c + 128] * (txt_b[part, :] + all_a[0, :, c:c + 128]) for c in range(j * 512, (j + 1) * 512, 128)]
            g = jnp.concatenate([v.astype(BF16) for v in g], axis=1)
            more = jnp.dot(g, img_p[j * 512:(j + 1) * 512, :], preferred_element_type=F32)
            total = more if total is None else total + more
        d_txt_acc[part, :] += total
        return carry
    lax.fori_loop(0, STEPS, partner_body, 0)

    def outside(own, own_factor, others, factor, total):
        dots = lax.dot_general(own, others, (((1,), (1,)), ((), ())), preferred_element_type=F32)
        e = jnp.exp2(dots * scale2)
        g = [(e[:, c:c + 128] * (own_factor + factor[:, c:c + 128])).astype(BF16) for c in range(0, others.shape[0], 128)]
        total[...] += jnp.dot(jnp.concatenate(g, axis=1), others, preferred_element_type=F32)

    def both_sides(start, size):
        part = pl.ds(start, size)
        outside(txt[0], txt_b[...], new_img[part, :], new_a[:, part], d_txt_acc)
        outside(img[0:ROWS, :], row_a[0:ROWS, :], new_txt[part, :], new_b[:, part], d_img_acc)

    def relays(k, dst, size):
        direct, relayed = pl.ds(dst, size), pl.ds(dst + size, size)
        rx = to_row(new_img_pieces.at[direct], new_img_pieces.at[relayed], fx_send.at[k], fx_recv.at[k], partner)
        ry = to_row(new_txt_pieces.at[direct], new_txt_pieces.at[relayed], fy_send.at[k], fy_recv.at[k], partner)
        return rx, ry

    def land(k, dst, size):
        direct = pl.ds(dst, size)
        rx, ry = relays(k, dst, size)
        to_row(new_img_pieces.at[direct], new_img_pieces.at[direct], bx_send.at[k], bx_recv.at[k], across).wait_recv()
        rx.start()
        to_y(new_txt_pieces.at[direct], new_txt_pieces.at[direct], by_send.at[k], by_recv.at[k]).wait_recv()
        ry.start()

    def relayed_in(k, dst, size):
        for copy in relays(k, dst, size):
            copy.wait_recv()

    def sent(k, dst, size):
        direct = pl.ds(dst, size)
        to_row(new_img_pieces.at[direct], new_img_pieces.at[direct], bx_send.at[k], bx_recv.at[k], across).wait_send()
        to_y(new_txt_pieces.at[direct], new_txt_pieces.at[direct], by_send.at[k], by_recv.at[k]).wait_send()
        for copy in relays(k, dst, size):
            copy.wait_send()

    def early_sent():
        for k in range(G_STEPS):
            gather_x[k].wait_send()
            gather_y[k].wait_send()
            relay[k].wait_send()
            relay_n[k].wait_send()
        for k in range(2):
            sent(k, *bulk_span(k)[1:])
        gather_p.wait_send()
        gather_i.wait_send()
        swap_b.wait_send()
        swap_row.wait_send()
        for t in range(3):
            swap_col[t].wait_send()
            send_s[t].wait_send()
            swap_a[t].wait_send()

    land(0, 0, 2)
    both_sides(0, CHUNK)
    land(1, 4, 1)
    relayed_in(0, 0, 2)
    both_sides(CHUNK, CHUNK + PIECE)
    land(2, 6, 2)
    relayed_in(1, 4, 1)
    both_sides(2 * CHUNK + PIECE, CHUNK + PIECE)

    def bulk_body(k, carry):
        @pl.when(k == 5)
        def _():
            early_sent()
        land(k, 4 * k - 2, 2)
        relayed_in(k - 1, 4 * k - 6, 2)
        sent(k - 1, 4 * k - 6, 2)
        both_sides(pl.multiple_of(2 * (k - 1) * CHUNK, CHUNK), 2 * CHUNK)
        return carry
    lax.fori_loop(3, BULK - 1, bulk_body, 0)

    src, dst, size = bulk_span(BULK - 1)
    land(BULK - 1, dst, size)
    relayed_in(BULK - 2, dst - 4, 2)
    both_sides(dst * PIECE - CHUNK, CHUNK + PIECE)
    relayed_in(BULK - 1, dst, size)
    both_sides((dst + 1) * PIECE, PIECE)

    dimg_ref[...] = (scale * d_img_acc[...]).astype(BF16)
    dtxt_ref[...] = (scale * d_txt_acc[...]).astype(BF16)

    swap_s.wait_recv()
    total = scal_y[0] + scal_y[1]
    loss_ref[0, 0] = total[0, 0]
    dscale_ref[0, 0] = total[0, 1]

    for k in range(BULK - 2, BULK):
        sent(k, *bulk_span(k)[1:])
    swap_s.wait_send()


def solution(mesh):
    batch_spec = P(("row", "col"), None)
    n_dev = mesh.shape["row"] * mesh.shape["col"]
    inv_count = 1.0 / (2 * ROWS * n_dev)
    dma = pltpu.SemaphoreType.DMA

    def local_tile(img_loc, txt_loc, log_scale):
        any_spec = pl.BlockSpec(memory_space=pl.ANY)
        vmem_spec = pl.BlockSpec(memory_space=pltpu.VMEM)
        smem_spec = pl.BlockSpec(memory_space=pltpu.SMEM)
        loss, d_img, d_txt, d_scale = pl.pallas_call(
            functools.partial(kernel, inv_count),
            out_shape=(
                jax.ShapeDtypeStruct((1, 1), F32),
                pltpu.VMEM((ROWS, DIM), BF16),
                pltpu.VMEM((ROWS, DIM), BF16),
                jax.ShapeDtypeStruct((1, 1), F32),
            ),
            in_specs=[smem_spec, any_spec, any_spec],
            out_specs=(smem_spec, vmem_spec, vmem_spec, smem_spec),
            scratch_shapes=[
                pltpu.VMEM((IMGS, DIM), BF16),
                pltpu.VMEM((2, ROWS, DIM), BF16),
                pltpu.VMEM((ROWS // PIECE, 2, PIECE, DIM), BF16),
                pltpu.VMEM((DIM, TXTS), BF16),
                pltpu.VMEM((IMGS, DIM), BF16),
                pltpu.VMEM((TXTS, DIM), BF16),
                pltpu.VMEM((TXTS, DIM), BF16),
                pltpu.VMEM((IMGS, TXTS), F32),
                pltpu.VMEM((IMGS, 128), F32),
                pltpu.VMEM((IMGS, 128), F32),
                pltpu.VMEM((8, TXTS), F32),
                pltpu.VMEM((8, TXTS), F32),
                pltpu.VMEM((1, IMGS), F32),
                pltpu.VMEM((1, IMGS), F32),
                pltpu.VMEM((1, TXTS), F32),
                pltpu.VMEM((3, 1, TXTS), F32),
                pltpu.VMEM((1, TXTS), F32),
                pltpu.VMEM((1, IMGS), F32),
                pltpu.VMEM((3, 1, IMGS), F32),
                pltpu.VMEM((1, TXTS), F32),
                pltpu.VMEM((1, TXTS), F32),
                pltpu.VMEM((1, TXTS), F32),
                pltpu.VMEM((ROWS, 128), F32),
                pltpu.VMEM((4, 8, 128), F32),
                pltpu.VMEM((2, 8, 128), F32),
                dma((2 * G_STEPS,)),
                dma((G_STEPS,)), dma((G_STEPS,)),
                dma((G_STEPS,)), dma((G_STEPS,)),
                dma((4,)),
                dma((G_STEPS,)), dma((G_STEPS,)),
                dma((2,)),
                dma((3,)), dma((3,)),
                dma((BULK,)), dma((BULK,)), dma((BULK,)), dma((BULK,)),
                dma((BULK,)), dma((BULK,)), dma((BULK,)), dma((BULK,)),
                dma((G_STEPS,)), dma((G_STEPS,)),
                dma((3,)), dma((3,)), dma((2,)),
                dma((4,)), dma((4,)),
            ],
            compiler_params=pltpu.CompilerParams(
                collective_id=0, has_side_effects=True, vmem_limit_bytes=VMEM_LIMIT,
            ),
            name="clip_loss",
        )(log_scale.reshape(1, 1), img_loc, txt_loc)
        return loss.reshape(()), d_img, d_txt, d_scale.reshape(())

    return jax.shard_map(local_tile, mesh=mesh, in_specs=(batch_spec, batch_spec, P()), out_specs=(P(), batch_spec, batch_spec, P()), check_vma=False)
```

profile of v0, /device:TPU:0, one launch (start us, length us, event | category | flops | bytes accessed | tf_op | source)
XLA Modules:
  0.0 87.3 jit_solution(5621623342009617369)
XLA Ops:
  1.3 80.7 %clip_loss.1 = (f32[1,1]{1,0:T(1,128)}, bf16[1024,512]{1,0:T(8,128)(2,1)S(1)}, bf16[1024,512]{1,0:T(8,128)(2,1)S(1)}, f32[1,1]{1,0:T(1,128)}) custom-call(f32[1,1]{1,0:T(1,128)} %bitcast.3.scale_ref, bf16[1024,512]{1,0:T(8,128)(2,1)} %img_hbm.1, bf16[1024,512]{1,0:T(8,128)(2,1)} %txt_hbm.1), custom_call_target="tpu_custom_call" | custom-call | tf_op jit(solution)/shard_map/clip_loss/pallas_call | solution.py:429
  81.9 1.0 %copy.11 = bf16[1024,512]{1,0:T(8,128)(2,1)} copy(bf16[1024,512]{1,0:T(8,128)(2,1)S(1)} %get-tuple-element.13) | data formatting | bytes 2097152
  82.9 1.0 %copy.12 = bf16[1024,512]{1,0:T(8,128)(2,1)} copy(bf16[1024,512]{1,0:T(8,128)(2,1)S(1)} %get-tuple-element.14) | data formatting | bytes 2097152
where the time goes:
time: 87.5 us; the launch traced here: 87.3 us
  Pallas kernels  80.7 us (92%)
  between operations  4.74 us (5%)
  local copies, waits for them, and re-layouts  1.94 us (2%)
    pallas_call x1, Pallas kernels, local_tile(): pl.pallas_call(functools.partial(kernel, inv_count), out_shape=(jax.Shape...  80.7 us
    unnamed x2, local copies, waits for them, and re-layouts  1.94 us

commit v1 on v0

--- a/solution.py
+++ b/solution.py
@@ -10,6 +10,7 @@
 
 MESH = pl.DeviceIdType.MESH
 VMEM_LIMIT = 247 * 256 * 1024
+MARGIN = 4 * 1024 * 1024
 F32 = jnp.float32
 BF16 = jnp.bfloat16
 ROWS = 1024
@@ -29,7 +30,7 @@
 LOG2E = math.log2(math.e)
 
 
-def kernel(inv_count, scale_ref, img_hbm, txt_hbm, loss_ref, dimg_ref, dtxt_ref, dscale_ref,
+def kernel(inv_count, scale_ref, img_hbm, txt_hbm, scal_ref, dimg_ref, dtxt_ref,
            img, txt, far, txt_t, img_p, new_txt, new_img, exps, row_e, row_m, col_e, col_m, row_send, row_recv, col_send, col_recv, col_b, row_l, all_a, all_b, new_a, new_b, txt_b,
            scal, scal_y, load_sem, gy_send, gy_recv, gx_send, gx_recv, gp_sem, gf_send, gf_recv, row_sem, col_ssem, col_rsem,
            bx_send, bx_recv, by_send, by_recv, fx_send, fx_recv, fy_send, fy_recv, pn_send, pn_recv,
@@ -321,7 +322,6 @@
             total = more if total is None else total + more
         d_txt_acc[part, :] += total
         return carry
-    lax.fori_loop(0, STEPS, partner_body, 0)
 
     def outside(own, own_factor, others, factor, total):
         dots = lax.dot_general(own, others, (((1,), (1,)), ((), ())), preferred_element_type=F32)
@@ -376,25 +376,24 @@
             send_s[t].wait_send()
             swap_a[t].wait_send()
 
-    land(0, 0, 2)
-    both_sides(0, CHUNK)
-    land(1, 4, 1)
-    relayed_in(0, 0, 2)
-    both_sides(CHUNK, CHUNK + PIECE)
-    land(2, 6, 2)
-    relayed_in(1, 4, 1)
-    both_sides(2 * CHUNK + PIECE, CHUNK + PIECE)
+    for k in range(3):
+        land(k, *bulk_span(k)[1:])
+    lax.fori_loop(0, STEPS, partner_body, 0)
+    for k in range(2):
+        relayed_in(k, *bulk_span(k)[1:])
 
     def bulk_body(k, carry):
         @pl.when(k == 5)
         def _():
             early_sent()
-        land(k, 4 * k - 2, 2)
-        relayed_in(k - 1, 4 * k - 6, 2)
-        sent(k - 1, 4 * k - 6, 2)
+        @pl.when(k >= 3)
+        def _():
+            land(k, 4 * k - 2, 2)
+            relayed_in(k - 1, 4 * k - 6, 2)
+            sent(k - 1, 4 * k - 6, 2)
         both_sides(pl.multiple_of(2 * (k - 1) * CHUNK, CHUNK), 2 * CHUNK)
         return carry
-    lax.fori_loop(3, BULK - 1, bulk_body, 0)
+    lax.fori_loop(1, BULK - 1, bulk_body, 0)
 
     src, dst, size = bulk_span(BULK - 1)
     land(BULK - 1, dst, size)
@@ -407,13 +406,24 @@
     dtxt_ref[...] = (scale * d_txt_acc[...]).astype(BF16)
 
     swap_s.wait_recv()
-    total = scal_y[0] + scal_y[1]
-    loss_ref[0, 0] = total[0, 0]
-    dscale_ref[0, 0] = total[0, 1]
+    scal_ref[...] = scal_y[0] + scal_y[1]
 
     for k in range(BULK - 2, BULK):
         sent(k, *bulk_span(k)[1:])
     swap_s.wait_send()
+
+
+def put_kernel(scal_in, img_in, txt_in, loss_out, img_out, txt_out, dscale_out, loss_cell, dscale_cell, sems):
+    copies = [pltpu.make_async_copy(img_in, img_out, sems.at[0]), pltpu.make_async_copy(txt_in, txt_out, sems.at[1])]
+    for copy in copies:
+        copy.start()
+    loss_cell[0, 0] = scal_in[0, 0]
+    dscale_cell[0, 0] = scal_in[0, 1]
+    cells = [pltpu.make_async_copy(loss_cell, loss_out, sems.at[2]), pltpu.make_async_copy(dscale_cell, dscale_out, sems.at[3])]
+    for copy in cells:
+        copy.start()
+    for copy in copies + cells:
+        copy.wait()
 
 
 def solution(mesh):
@@ -426,16 +436,15 @@
         any_spec = pl.BlockSpec(memory_space=pl.ANY)
         vmem_spec = pl.BlockSpec(memory_space=pltpu.VMEM)
         smem_spec = pl.BlockSpec(memory_space=pltpu.SMEM)
-        loss, d_img, d_txt, d_scale = pl.pallas_call(
+        scalars, d_img, d_txt = pl.pallas_call(
             functools.partial(kernel, inv_count),
             out_shape=(
-                jax.ShapeDtypeStruct((1, 1), F32),
+                pltpu.VMEM((8, 128), F32),
                 pltpu.VMEM((ROWS, DIM), BF16),
                 pltpu.VMEM((ROWS, DIM), BF16),
-                jax.ShapeDtypeStruct((1, 1), F32),
             ),
             in_specs=[smem_spec, any_spec, any_spec],
-            out_specs=(smem_spec, vmem_spec, vmem_spec, smem_spec),
+            out_specs=(vmem_spec, vmem_spec, vmem_spec),
             scratch_shapes=[
                 pltpu.VMEM((IMGS, DIM), BF16),
                 pltpu.VMEM((2, ROWS, DIM), BF16),
@@ -480,6 +489,17 @@
             ),
             name="clip_loss",
         )(log_scale.reshape(1, 1), img_loc, txt_loc)
+        rows_shape = jax.ShapeDtypeStruct((ROWS, DIM), BF16)
+        cell_shape = jax.ShapeDtypeStruct((1, 1), F32)
+        loss, d_img, d_txt, d_scale = pl.pallas_call(
+            put_kernel,
+            out_shape=(cell_shape, rows_shape, rows_shape, cell_shape),
+            in_specs=[vmem_spec, vmem_spec, vmem_spec],
+            out_specs=(any_spec, any_spec, any_spec, any_spec),
+            scratch_shapes=[pltpu.SMEM((1, 1), F32), pltpu.SMEM((1, 1), F32), dma((4,))],
+            compiler_params=pltpu.CompilerParams(vmem_limit_bytes=MARGIN),
+            name="put_rows",
+        )(scalars, d_img, d_txt)
         return loss.reshape(()), d_img, d_txt, d_scale.reshape(())
 
     return jax.shard_map(local_tile, mesh=mesh, in_specs=(batch_spec, batch_spec, P()), out_specs=(P(), batch_spec, batch_spec, P()), check_vma=False)

time: 87.5 us -> 83 us (0.949)
  between operations: 4.74 us -> 1.45 us
  local copies, waits for them, and re-layouts: 1.94 us -> 0 us
    unnamed x2 -> x0, local copies, waits for them, and re-layouts: 1.94 us -> none
    pallas_call x1 -> x2, Pallas kernels: 80.7 us -> 81.4 us  [the longest x1 80 us: local_tile(): pl.pallas_call(functools.partial(kernel, inv_count), out_shape=(pltpu.VME...]
where the time goes in v1:
time: 83 us; the launch traced here: 82.8 us
  Pallas kernels  81.4 us (98%)
  between operations  1.45 us (2%)
    pallas_call x1, Pallas kernels, local_tile(): pl.pallas_call(functools.partial(kernel, inv_count), out_shape=(pltpu.VME...  80 us

profile of v1, /device:TPU:0, one launch (start us, length us, event | category | flops | bytes accessed | tf_op | source)
XLA Modules:
  0.0 82.8 jit_solution(2590195362863576796)
XLA Ops:
  1.3 80.0 %clip_loss.1 = (f32[8,128]{1,0:T(8,128)S(1)}, bf16[1024,512]{1,0:T(8,128)(2,1)S(1)}, bf16[1024,512]{1,0:T(8,128)(2,1)S(1)}) custom-call(f32[1,1]{1,0:T(1,128)} %bitcast.3.scale_ref, bf16[1024,512]{1,0:T(8,128)(2,1)} %img_hbm.1, bf16[1024,512]{1,0:T(8,128)(2,1)} %txt_hbm.1), custom_call_target="tpu_custom_call" | custom-call | tf_op jit(solution)/shard_map/clip_loss/pallas_call | solution.py:439
  81.3 1.4 %put_rows.1 = (f32[1,1]{1,0:T(1,128)}, bf16[1024,512]{1,0:T(8,128)(2,1)}, bf16[1024,512]{1,0:T(8,128)(2,1)}, f32[1,1]{1,0:T(1,128)}) custom-call(f32[8,128]{1,0:T(8,128)S(1)} %get-tuple-element.11.scal_in, bf16[1024,512]{1,0:T(8,128)(2,1)S(1)} %get-tuple-element.12.img_in, bf16[1024,512]{1,0:T(8,128)(2,1)S(1)} %get-tuple-element.13.txt_in), custom_call_target="tpu_custom_call" | custom-call | tf_op jit(solution)/shard_map/put_rows/pallas_call | solution.py:494
